TPU v7x, 32 devices: a whole 2x2x4 slice. The times are simulated.
32 devices in a mesh: dp: 8 (over y, x, core), tensor: 4 (over z).
Axes of the slice: x: 2, y: 2, z: 4, core: 2. Of those that a mesh axis runs over, the one named last changes fastest.
Arguments:
- images: bfloat16 [32, 320, 1024], P('dp', None, 'tensor'), may hold values from -6 to 6
- lengths: int32 [32], P('dp'), may hold values from 224 to 320, as said below
- cotangent: bfloat16 [32, 320, 1024], P('dp', None, 'tensor'), may hold values from -6 to 6
- norm1_gain: float32 [1024], replicated, may hold values from 0.5 to 1.5
- norm1_shift: float32 [1024], replicated, may hold values from -1.75 to 1.75
- w_qkv: bfloat16 [1024, 3, 1024], P(None, None, 'tensor'), may hold values from -0.1875 to 0.1875
- qv_bias: float32 [2, 1024], P(None, 'tensor'), may hold values from -3 to 3
- w_proj: bfloat16 [1024, 1024], P('tensor'), may hold values from -1.5 to 1.5
- proj_bias: float32 [1024], replicated, may hold values from -3 to 3
- norm2_gain: float32 [1024], replicated, may hold values from 0.5 to 1.5
- norm2_shift: float32 [1024], replicated, may hold values from -1.75 to 1.75
- w_fc1: bfloat16 [1024, 4096], P(None, 'tensor'), may hold values from -0.1875 to 0.1875
- fc1_bias: float32 [4096], P('tensor'), may hold values from -3 to 3
- w_fc2: bfloat16 [4096, 1024], P('tensor'), may hold values from -0.09375 to 0.09375
- fc2_bias: float32 [1024], replicated, may hold values from -3 to 3
Outputs:
- output: bfloat16 [32, 320, 1024], P('dp', None, 'tensor')
- input_grad: bfloat16 [32, 320, 1024], P('dp', None, 'tensor')
- grad_norm1_gain: float32 [1024], replicated
- grad_norm1_shift: float32 [1024], replicated
- grad_w_qkv: float32 [1024, 3, 1024], P(None, None, 'tensor')
- grad_qv_bias: float32 [2, 1024], P(None, 'tensor')
- grad_w_proj: float32 [1024, 1024], P('tensor')
- grad_proj_bias: float32 [1024], replicated
- grad_norm2_gain: float32 [1024], replicated
- grad_norm2_shift: float32 [1024], replicated
- grad_w_fc1: float32 [1024, 4096], P(None, 'tensor')
- grad_fc1_bias: float32 [4096], P('tensor')
- grad_w_fc2: float32 [4096, 1024], P('tensor')
- grad_fc2_bias: float32 [1024], replicated
Inputs may be any that keep to these rules, and one draw needn't show every extreme that they name: lengths[i] is the number of valid slots of image i, which come first; some image has all 320 slots valid in every draw.
All inputs are finite; a program needn't handle non-finite values.
Results may differ from a plain program's by a relative error of at most 0.02.
Values may be sent and summed in bfloat16 or wider, within the bound.
A program may use at most 192 MiB of HBM per device.

v0:
```python
import jax
import jax.numpy as jnp
from jax import lax
from jax.sharding import PartitionSpec as P

HEAD_DIM = 64


EPS = 1e-06
MASKED = -1e30


def norm_rows(values, gain_row, shift_row):
    row_mean = jnp.mean(values, axis=-1, keepdims=True)
    centered = values - row_mean
    spread = jnp.mean(centered * centered, axis=-1, keepdims=True)
    inverse = lax.rsqrt(spread + EPS)
    unit_rows = centered * inverse
    return (unit_rows * gain_row + shift_row, unit_rows, inverse)


def norm_back(gradient, unit_rows, inverse, gain_row):
    scaled = gradient * gain_row
    first_mean = jnp.mean(scaled, axis=-1, keepdims=True)
    cross_mean = jnp.mean(scaled * unit_rows, axis=-1, keepdims=True)
    return inverse * (scaled - first_mean - unit_rows * cross_mean)


def scores_of(queries, key_heads, key_mask, score_scale):
    raw_scores = (
        jnp.einsum("bqhe,bkhe->bhqk", queries, key_heads, preferred_element_type=jnp.float32)
        * score_scale
    )
    return jnp.where(key_mask, raw_scores, MASKED)


def exact_gelu(values):
    return jax.nn.gelu(values, approximate=False)


def per_device(
    images,
    lengths,
    cotangent,
    norm1_gain,
    norm1_shift,
    w_qkv,
    qv_bias,
    w_proj,
    proj_bias,
    norm2_gain,
    norm2_shift,
    w_fc1,
    fc1_bias,
    w_fc2,
    fc2_bias,
):
    images_here, slot_count, col_count = images.shape
    model_width = w_qkv.shape[0]
    local_width = w_qkv.shape[2]
    heads_here = local_width // HEAD_DIM
    row_count = images_here * slot_count
    score_scale = HEAD_DIM ** (-0.5)
    first_col = lax.axis_index("tensor") * col_count
    full_images, full_cot = (
        lax.all_gather(images, "tensor", axis=2, tiled=True),
        lax.all_gather(cotangent, "tensor", axis=2, tiled=True),
    )
    slot_ids = jnp.arange(slot_count, dtype=jnp.int32)
    valid_slots = (slot_ids[None, :] < lengths[:, None]).astype(jnp.float32)
    keep_rows = valid_slots.reshape(row_count, 1)
    row_values = full_images.reshape(row_count, model_width).astype(jnp.float32) * keep_rows
    normed1, unit1, inverse1 = norm_rows(row_values, norm1_gain, norm1_shift)
    normed1 = normed1.astype(jnp.bfloat16)
    qkv_bias = jnp.concatenate([qv_bias[0], jnp.zeros_like(qv_bias[0]), qv_bias[1]])
    w_flat = w_qkv.reshape(model_width, 3 * local_width)
    qkv_rows = (jnp.dot(normed1, w_flat, preferred_element_type=jnp.float32) + qkv_bias).astype(
        jnp.bfloat16
    )
    qkv_rows = qkv_rows.reshape(images_here, slot_count, 3, heads_here, HEAD_DIM)
    queries = qkv_rows[:, :, 0]
    key_heads = qkv_rows[:, :, 1]
    value_heads = qkv_rows[:, :, 2]
    key_mask = valid_slots[:, None, None, :] > 0
    scores = scores_of(queries, key_heads, key_mask, score_scale)
    row_top = jnp.max(scores, axis=-1, keepdims=True)
    shifted = jnp.exp(scores - row_top)
    row_total = jnp.sum(shifted, axis=-1, keepdims=True)
    probability = (shifted / row_total).astype(jnp.bfloat16)
    log_total = row_top + jnp.log(row_total)
    mixed = jnp.einsum(
        "bhqk,bkhe->bqhe", probability, value_heads, preferred_element_type=jnp.float32
    ).astype(jnp.bfloat16)
    mixed_rows = mixed.reshape(row_count, local_width)
    attn_part = jnp.dot(mixed_rows, w_proj, preferred_element_type=jnp.float32)
    middle = (
        row_values
        + lax.psum(attn_part.astype(jnp.bfloat16), "tensor").astype(jnp.float32)
        + proj_bias
    )
    normed2, unit2, inverse2 = norm_rows(middle, norm2_gain, norm2_shift)
    normed2 = normed2.astype(jnp.bfloat16)
    pre_act = jnp.dot(normed2, w_fc1, preferred_element_type=jnp.float32) + fc1_bias
    activated = exact_gelu(pre_act).astype(jnp.bfloat16)
    ff_part = jnp.dot(activated, w_fc2, preferred_element_type=jnp.float32)
    ff_share = lax.psum_scatter(
        ff_part.astype(jnp.bfloat16), "tensor", scatter_dimension=1, tiled=True
    ).astype(jnp.float32)
    middle_cols = lax.dynamic_slice_in_dim(middle, first_col, col_count, 1)
    bias_cols = lax.dynamic_slice_in_dim(fc2_bias, first_col, col_count, 0)
    output = ((middle_cols + ff_share + bias_cols) * keep_rows).astype(jnp.bfloat16)
    output = output.reshape(images_here, slot_count, col_count)
    grad_out = full_cot.reshape(row_count, model_width).astype(jnp.float32) * keep_rows
    grad_ff = grad_out.astype(jnp.bfloat16)
    grad_fc2_bias = jnp.sum(grad_ff, axis=0, dtype=jnp.float32)
    grad_w_fc2 = jnp.einsum("rf,rd->fd", activated, grad_ff, preferred_element_type=jnp.float32)
    grad_act = jnp.einsum("rd,fd->rf", grad_ff, w_fc2, preferred_element_type=jnp.float32)
    gelu_pull = jax.vjp(exact_gelu, pre_act)[1]
    grad_pre = gelu_pull(grad_act)[0].astype(jnp.bfloat16)
    grad_fc1_bias = jnp.sum(grad_pre, axis=0, dtype=jnp.float32)
    grad_w_fc1 = jnp.einsum("rd,rf->df", normed2, grad_pre, preferred_element_type=jnp.float32)
    hidden_part = jnp.einsum("rf,df->rd", grad_pre, w_fc1, preferred_element_type=jnp.float32)
    grad_normed2 = lax.psum(hidden_part.astype(jnp.bfloat16), "tensor").astype(jnp.float32)
    grad_norm2_gain = jnp.sum(grad_normed2 * unit2, axis=0)
    grad_norm2_shift = jnp.sum(grad_normed2, axis=0)
    grad_middle = grad_out + norm_back(grad_normed2, unit2, inverse2, norm2_gain)
    grad_attn = grad_middle.astype(jnp.bfloat16)
    grad_proj_bias = jnp.sum(grad_attn, axis=0, dtype=jnp.float32)
    grad_w_proj = jnp.einsum("rc,rd->cd", mixed_rows, grad_attn, preferred_element_type=jnp.float32)
    grad_mixed = jnp.einsum(
        "rd,cd->rc", grad_attn, w_proj, preferred_element_type=jnp.float32
    ).astype(jnp.bfloat16)
    grad_mixed = grad_mixed.reshape(images_here, slot_count, heads_here, HEAD_DIM)
    scores_again = scores_of(queries, key_heads, key_mask, score_scale)
    weights_soft = jnp.exp(scores_again - log_total)
    grad_value = jnp.einsum(
        "bhqk,bqhe->bkhe",
        weights_soft.astype(jnp.bfloat16),
        grad_mixed,
        preferred_element_type=jnp.float32,
    )
    grad_prob = jnp.einsum(
        "bqhe,bkhe->bhqk", grad_mixed, value_heads, preferred_element_type=jnp.float32
    )
    row_dot = jnp.sum(weights_soft * grad_prob, axis=-1, keepdims=True)
    grad_scores = (weights_soft * (grad_prob - row_dot)).astype(jnp.bfloat16)
    grad_query = (
        jnp.einsum("bhqk,bkhe->bqhe", grad_scores, key_heads, preferred_element_type=jnp.float32)
        * score_scale
    )
    grad_key = (
        jnp.einsum("bhqk,bqhe->bkhe", grad_scores, queries, preferred_element_type=jnp.float32)
        * score_scale
    )
    grad_qkv = jnp.stack([grad_query, grad_key, grad_value], axis=2).astype(jnp.bfloat16)
    grad_qkv = grad_qkv.reshape(row_count, 3 * local_width)
    bias_sums = jnp.sum(grad_qkv, axis=0, dtype=jnp.float32).reshape(3, local_width)
    grad_qv_bias = jnp.stack([bias_sums[0], bias_sums[2]])
    grad_w_qkv = jnp.einsum("rd,rc->dc", normed1, grad_qkv, preferred_element_type=jnp.float32)
    grad_w_qkv = grad_w_qkv.reshape(model_width, 3, local_width)
    normed_part = jnp.einsum("rc,dc->rd", grad_qkv, w_flat, preferred_element_type=jnp.float32)
    grad_normed1 = lax.psum(normed_part.astype(jnp.bfloat16), "tensor").astype(jnp.float32)
    grad_norm1_gain = jnp.sum(grad_normed1 * unit1, axis=0)
    grad_norm1_shift = jnp.sum(grad_normed1, axis=0)
    grad_full = grad_middle + norm_back(grad_normed1, unit1, inverse1, norm1_gain)
    grad_input = lax.dynamic_slice_in_dim(grad_full, first_col, col_count, 1) * keep_rows
    input_grad = grad_input.astype(jnp.bfloat16).reshape(images_here, slot_count, col_count)
    summed = (
        lax.psum(grad_norm1_gain.astype(jnp.bfloat16), "dp").astype(jnp.float32),
        lax.psum(grad_norm1_shift.astype(jnp.bfloat16), "dp").astype(jnp.float32),
        lax.psum(grad_w_qkv.astype(jnp.bfloat16), "dp").astype(jnp.float32),
        lax.psum(grad_qv_bias.astype(jnp.bfloat16), "dp").astype(jnp.float32),
        lax.psum(grad_w_proj.astype(jnp.bfloat16), "dp").astype(jnp.float32),
        lax.psum(grad_proj_bias.astype(jnp.bfloat16), "dp").astype(jnp.float32),
        lax.psum(grad_norm2_gain.astype(jnp.bfloat16), "dp").astype(jnp.float32),
        lax.psum(grad_norm2_shift.astype(jnp.bfloat16), "dp").astype(jnp.float32),
        lax.psum(grad_w_fc1.astype(jnp.bfloat16), "dp").astype(jnp.float32),
        lax.psum(grad_fc1_bias.astype(jnp.bfloat16), "dp").astype(jnp.float32),
        lax.psum(grad_w_fc2.astype(jnp.bfloat16), "dp").astype(jnp.float32),
        lax.psum(grad_fc2_bias.astype(jnp.bfloat16), "dp").astype(jnp.float32),
    )
    return (
        output,
        input_grad,
        summed[0],
        summed[1],
        summed[2],
        summed[3],
        summed[4],
        summed[5],
        summed[6],
        summed[7],
        summed[8],
        summed[9],
        summed[10],
        summed[11],
    )


def solution(mesh):
    in_specs = (
        P("dp", None, "tensor"),
        P("dp"),
        P("dp", None, "tensor"),
        P(),
        P(),
        P(None, None, "tensor"),
        P(None, "tensor"),
        P("tensor", None),
        P(),
        P(),
        P(),
        P(None, "tensor"),
        P("tensor"),
        P("tensor", None),
        P(),
    )
    out_specs = (
        P("dp", None, "tensor"),
        P("dp", None, "tensor"),
        P(),
        P(),
        P(None, None, "tensor"),
        P(None, "tensor"),
        P("tensor", None),
        P(),
        P(),
        P(),
        P(None, "tensor"),
        P("tensor"),
        P("tensor", None),
        P(),
    )
    return jax.shard_map(
        per_device, mesh=mesh, in_specs=in_specs, out_specs=out_specs, check_vma=False
    )
```

profile of v0, /device:TPU:0, one launch (start us, length us, event | category | flops | bytes accessed | tf_op | source)
XLA Modules:
  0.0 699.4 jit_solution(9213317824829638723)
XLA Ops:
  8.7 0.8 fusion.59
  10.2 2.6 copy.39
  12.8 54.3 %all-gather.3.cloned.1.call-done = bf16[4,320,1024]{2,1,0:T(8,128)(2,1)} async-done(((bf16[4,320,256]{2,1,0:T(8,128)(2,1)}), bf16[4,320,1024]{2,1,0:T(8,128)(2,1)}) %all-gather.3.cloned.1.call-update) | async-done | bytes 2621456 | tf_op jit(solution)/shard_map/all_gather | solution.py:66
  67.2 2.6 fusion.18
  69.8 2.8 multiply_reduce_fusion.3
  72.6 1.3 add_convert_fusion.2
  73.9 1.5 copy-done.13
  75.4 3.5 add_convert_fusion.3
  78.9 6.7 reshape.265
  85.6 4.0 fusion.57
  89.6 2.3 copy.64
  91.8 2.5 copy.65
  94.3 3.2 copy.66
  97.5 3.2 fusion.24
  100.8 1.9 fusion
  102.7 2.4 fusion.35
  105.2 1.5 copy.45
  106.7 2.3 reshape.257
  109.0 3.4 convolution_convert_fusion.1
  112.6 9.2 %all-gather.5.cloned.1.call-done = bf16[4,320,1024]{2,1,0:T(8,128)(2,1)} async-done(((bf16[4,320,256]{2,1,0:T(8,128)(2,1)}), bf16[4,320,1024]{2,1,0:T(8,128)(2,1)}) %all-gather.5.cloned.1.call-update) | async-done | bytes 2621456 | tf_op jit(solution)/shard_map/all_gather | solution.py:67
  121.8 105.2 %all-reduce.7.cloned.1.call-done = bf16[1280,1024]{1,0:T(8,128)(2,1)} async-done(((bf16[1280,1024]{1,0:T(8,128)(2,1)}), bf16[1280,1024]{1,0:T(8,128)(2,1)}) %all-reduce.7.cloned.1.call-update) | async-done | bytes 2621456 | tf_op jit(solution)/shard_map/psum | solution.py:98
  227.0 5.0 fusion.56
  232.8 2.5 copy-done.48
  235.3 3.0 fusion.51
  238.4 16.8 %fusion.52 = (bf16[1024]{0:T(1024)(128)(2,1)}, bf16[1280,1024]{1,0:T(8,128)(2,1)S(1)}, f32[1280,1024]{1,0:T(8,128)}) fusion(f32[1280,1024]{1,0:T(8,128)S(1)} %fusion.51, f32[1024]{0:T(1024)S(1)} %copy-done.45, bf16[1280,1024]{1,0:T(8,128)(2,1)S(1)} %get-tuple-element.49, bf16[1024,1024]{1,0:T(8,128)(2,1)S(1)} %copy-done), kind=kOutput, calls=%fused_computation.113 | convolution fusion | flops 2781346816 | bytes 17831936 | tf_op jit(solution)/shard_map/rd,fd->rf/dot_general | solution.py:117
  255.2 1.5 copy-done.51
  256.6 4.2 convolution_convert_fusion.2
  260.9 1.4 log_add_fusion
  262.3 101.8 %all-reduce.9.cloned.1.call-done = bf16[1280,1024]{1,0:T(8,128)(2,1)} async-done(((bf16[1280,1024]{1,0:T(8,128)(2,1)}), bf16[1280,1024]{1,0:T(8,128)(2,1)}) %all-reduce.9.cloned.1.call-update) | async-done | bytes 2621456 | tf_op jit(solution)/shard_map/psum | solution.py:123
  364.1 5.4 fusion.9
  369.6 5.6 convert_reduce_fusion
  375.2 2.3 copy-done.4
  377.4 1.7 convolution_convert_fusion.4
  379.1 3.1 reshape.266
  382.2 3.2 copy.47
  385.5 5.5 fusion.27
  391.0 5.4 multiply_reduce_fusion
  396.5 2.7 multiply_convert_fusion
  399.2 1.3 multiply_bitcast_fusion
  400.6 0.9 multiply_bitcast_fusion.1
  402.0 3.2 copy.52
  405.2 4.7 convert_element_type.226
  409.9 5.7 convolution_convert_fusion
  415.8 5.5 multiply_convert_fusion.2
  421.2 1.5 copy-done.15
  422.7 4.1 convolution_convert_fusion.3
  427.2 7.1 %convolution_convert_fusion.5 = bf16[1024,1024]{1,0:T(8,128)(2,1)} fusion(bf16[1280,1024]{1,0:T(8,128)(2,1)} %copy-done.15, bf16[1280,1024]{1,0:T(8,128)(2,1)} %copy-done.12), kind=kOutput, calls=%fused_computation.66 | convolution fusion | flops 2685403136 | bytes 7340032 | tf_op jit(solution)/shard_map/rf,rd->fd/dot_general | solution.py:116
  434.3 7.3 %convolution_convert_fusion.6 = bf16[1024,1024]{1,0:T(8,128)(2,1)} fusion(bf16[1280,1024]{1,0:T(8,128)(2,1)S(1)} %copy-done.52, f32[1280,1024]{1,0:T(8,128)} %copy-done.2, f32[1024]{0:T(1024)S(1)} %copy-done.50, f32[1024]{0:T(1024)S(1)} %copy-done.38, f32[1280]{0:T(1024)S(1)} %copy-done.31, f32[1280]{0:T(1024)S(1)} %copy-done.25), kind=kOutput, calls=%fused_computation.67 | convolution fusion | flops 2691956736 | bytes 9979904 | tf_op jit(solution)/shard_map/rd,rf->df/dot_general | solution.py:121
  441.7 1.6 convolution_convert_fusion.8
  443.4 0.8 copy-done.19
  444.2 3.4 convolution_convert_fusion.7
  447.7 0.8 dynamic_slice.10
  448.6 2.4 fusion.25
  451.1 67.8 %all-reduce.11.cloned.1.call-done = bf16[1280,1024]{1,0:T(8,128)(2,1)} async-done(((bf16[1280,1024]{1,0:T(8,128)(2,1)}), bf16[1280,1024]{1,0:T(8,128)(2,1)}) %all-reduce.11.cloned.1.call-update) | async-done | bytes 2621456 | tf_op jit(solution)/shard_map/psum | solution.py:162
  519.0 2.2 reduce_sum.188
  521.2 7.4 %fusion.10 = (bf16[1024]{0:T(1024)(128)(2,1)S(1)}, f32[1280]{0:T(1024)S(1)}, f32[1280]{0:T(1024)S(1)}, f32[1280,1024]{1,0:T(8,128)}, f32[1280,1024]{1,0:T(8,128)}) fusion(bf16[1280,1024]{1,0:T(8,128)(2,1)} %all-reduce.11.cloned.1.call-done, f32[1280]{0:T(1024)S(1)} %rsqrt.22, f32[1280]{0:T(1024)S(1)} %div.43, f32[1280]{0:T(1024)S(1)} %reshape.262, ...), kind=kLoop, calls=%fused_computation.21 | loop fusion | flops 14414336 | bytes 15760384 | tf_op jit(solution)/shard_map/reduce_sum | solution.py:163
  528.7 24.7 %all-reduce = (bf16[1024]{0:T(1024)(128)(2,1)S(1)}, bf16[1024]{0:T(1024)(128)(2,1)S(1)}, bf16[2,256]{1,0:T(2,128)(2,1)S(1)}, bf16[1024]{0:T(1024)(128)(2,1)S(1)}...) all-reduce(bf16[1024]{0:T(1024)(128)(2,1)S(1)} %get-tuple-element.1, ...), channel_id=1, replica_groups=mesh['dp'=8,'tensor'=4] {'dp'}, use_global_device_ids=true, to_apply=%region_16.17 | all-reduce | flops 7680 | bytes 30720 | tf_op jit(solution)/shard_map/psum | solution.py:169
  558.1 14.9 %reduce-scatter.2.cloned.1.call-done = bf16[1280,256]{1,0:T(8,128)(2,1)} async-done(((bf16[1280,1024]{1,0:T(8,128)(2,1)}), bf16[1280,256]{1,0:T(8,128)(2,1)}) %reduce-scatter.2.cloned.1.call-update) | async-done | bytes 655376 | tf_op jit(solution)/shard_map/reduce_scatter | solution.py:106
  573.0 4.1 fusion.32
  577.1 104.3 %all-reduce.13.cloned.1.call-done = (bf16[1024,3,256]{2,0,1:T(8,128)(2,1)}, bf16[256,1024]{1,0:T(8,128)(2,1)}, bf16[1024,1024]{1,0:T(8,128)(2,1)}, bf16[1024,1024]{1,0:T(8,128)(2,1)}) async-done(((bf16[1024,3,256]{2,0,1:T(8,128)(2,1)}, bf16[256,1024]{1,0:T(8,128)(2,1)}, bf16[1024,1024]{1,0:T(8,128)(2,1)}, bf16[1024,1024]{1,0:T(8,128)(2,1)}), (bf16[1024,3,256]{2,0,1:T(8,128)(2,1)}, ...) | async-done | bytes 6291472 | tf_op jit(solution)/shard_map/psum | solution.py:171
  681.4 2.3 convert_element_type.238
  683.6 3.5 convert_element_type.234
  687.1 2.5 convert_element_type.244
  689.6 2.5 convert_element_type.247
  (151 shorter events, 9.5 us)
Async XLA Ops:
  7.2 231.2 %copy-start = (bf16[1024,1024]{1,0:T(8,128)(2,1)S(1)}, bf16[1024,1024]{1,0:T(8,128)(2,1)}, u32[]{:S(2)}) copy-start(bf16[1024,1024]{1,0:T(8,128)(2,1)} %param.28) | copy-start | bytes 6291460
  7.2 65.4 %copy-start.39 = (f32[1024]{0:T(1024)S(1)}, f32[1024]{0:T(1024)}, u32[]{:S(2)}) copy-start(f32[1024]{0:T(1024)} %param.18) | copy-start | bytes 12292
  7.2 65.3 %copy-start.44 = (f32[1024]{0:T(1024)S(1)}, f32[1024]{0:T(1024)}, u32[]{:S(2)}) copy-start(f32[1024]{0:T(1024)} %param.19) | copy-start | bytes 12292
  7.2 60.0 %all-gather.3.cloned.1.call-start = ((), (), s32[]{:S(2)}) async-start(), calls=%async_computation.1 | async-start | bytes 3276800 | tf_op jit(solution)/shard_map/all_gather | solution.py:66
  8.0 113.8 %all-gather.5.cloned.1.call-start = ((), (), s32[]{:S(2)}) async-start(), calls=%async_computation.4 | async-start | bytes 3276800 | tf_op jit(solution)/shard_map/all_gather | solution.py:67
  8.7 218.3 %all-reduce.7.cloned.1.call-start = ((), (), s32[]{:S(2)}) async-start(), calls=%async_computation.2 | async-start | bytes 5242880 | tf_op jit(solution)/shard_map/psum | solution.py:98
  10.2 92.5 %copy-start.34 = (pred[4,320]{1,0:T(4,128)(4,1)}, pred[4,320]{1,0:T(4,128)(4,1)S(1)}, u32[]{:S(2)}) copy-start(pred[4,320]{1,0:T(4,128)(4,1)S(1)} %get-tuple-element.54) | copy-start | bytes 3844
  67.2 5.4 copy-start.3
  67.2 8.2 %copy-start.20 = (bf16[1024,3,256]{0,2,1:T(8,128)(2,1)S(1)}, bf16[1024,3,256]{0,2,1:T(8,128)(2,1)}, u32[]{:S(2)}) copy-start(bf16[1024,3,256]{0,2,1:T(8,128)(2,1)} %copy.39) | copy-start | bytes 4718596
  69.7 4.1 copy-start.26
  72.6 1.3 copy-start.32
  73.9 1.5 copy-start.13
  100.7 4.4 copy-start.1
  100.7 4.4 copy-start.22
  100.8 1.9 copy-start.9
  102.7 2.5 copy-start.28
  112.5 251.6 %all-reduce.9.cloned.1.call-start = ((), (), s32[]{:S(2)}) async-start(), calls=%async_computation.5 | async-start | bytes 5242880 | tf_op jit(solution)/shard_map/psum | solution.py:123
  232.0 6.3 copy-start.2
  232.0 6.3 copy-start.12
  232.0 0.7 copy-start.36
  232.0 3.2 copy-start.48
  232.0 3.2 copy-start.49
  232.1 6.2 copy-start.23
  235.3 3.1 copy-start.29
  235.3 3.1 copy-start.45
  238.3 16.8 %copy-start.8 = (f32[1280,1024]{1,0:T(8,128)}, f32[1280,1024]{1,0:T(8,128)S(1)}, u32[]{:S(2)}) copy-start(f32[1280,1024]{1,0:T(8,128)S(1)} %fusion.51) | copy-start | bytes 15728644
  255.2 1.5 copy-start.51
  260.8 258.1 %all-reduce.11.cloned.1.call-start = ((), (), s32[]{:S(2)}) async-start(), calls=%async_computation.6 | async-start | bytes 5242880 | tf_op jit(solution)/shard_map/psum | solution.py:162
  364.1 5.5 copy-start.5
  364.1 5.5 copy-start.6
  364.1 5.5 copy-start.24
  364.1 5.5 copy-start.30
  364.1 5.5 copy-start.37
  369.6 7.8 %copy-start.18 = (bf16[256,1024]{1,0:T(8,128)(2,1)S(1)}, bf16[256,1024]{1,0:T(8,128)(2,1)}, u32[]{:S(2)}) copy-start(bf16[256,1024]{1,0:T(8,128)(2,1)} %param.22) | copy-start | bytes 1572868
  375.2 2.3 copy-start.4
  385.5 5.5 copy-start.10
  385.5 5.6 copy-start.11
  385.5 5.6 copy-start.21
  385.5 5.6 copy-start.35
  385.5 11.0 %slice-start = ((s8[7864320]{0:T(1024)(128)(4,1)}), s8[4194304]{0:T(1024)(128)(4,1)S(1)}, s32[]{:S(2)}) async-start(s8[7864320]{0:T(1024)(128)(4,1)} %bitcast.95), calls=%async_computation.8 | async-start | bytes 8388608
  391.0 5.4 slice-start.1
  399.2 1.4 copy-start.7
  409.9 5.8 copy-start.46
  415.7 157.3 %reduce-scatter.2.cloned.1.call-start = ((), (), s32[]{:S(2)}) async-start(), calls=%async_computation.3 | async-start | bytes 3276800 | tf_op jit(solution)/shard_map/reduce_scatter | solution.py:106
  421.2 1.5 copy-start.15
  426.9 7.4 %copy-start.25 = (f32[1280]{0:T(1024)S(1)}, f32[1280]{0:T(1024)}, u32[]{:S(2)}) copy-start(f32[1280]{0:T(1024)} %copy-done.23) | copy-start | bytes 15364
  426.9 7.4 %copy-start.31 = (f32[1280]{0:T(1024)S(1)}, f32[1280]{0:T(1024)}, u32[]{:S(2)}) copy-start(f32[1280]{0:T(1024)} %copy-done.29) | copy-start | bytes 15364
  426.9 7.4 %copy-start.38 = (f32[1024]{0:T(1024)S(1)}, f32[1024]{0:T(1024)}, u32[]{:S(2)}) copy-start(f32[1024]{0:T(1024)} %param.24) | copy-start | bytes 12292
  426.9 7.4 %copy-start.50 = (f32[1024]{0:T(1024)S(1)}, f32[1024]{0:T(1024)}, u32[]{:S(2)}) copy-start(f32[1024]{0:T(1024)} %param.25) | copy-start | bytes 12292
  426.9 254.4 %all-reduce.13.cloned.1.call-start = ((), (), s32[]{:S(2)}) async-start(), calls=%async_computation.7 | async-start | bytes 12582912 | tf_op jit(solution)/shard_map/psum | solution.py:171
  427.2 7.1 %copy-start.52 = (bf16[1280,1024]{1,0:T(8,128)(2,1)S(1)}, bf16[1280,1024]{1,0:T(8,128)(2,1)}, u32[]{:S(2)}) copy-start(bf16[1280,1024]{1,0:T(8,128)(2,1)} %copy-done.51) | copy-start | bytes 7864324
  427.2 14.4 %slice-start.2 = ((s8[5242880]{0:T(1024)(128)(4,1)}), s8[4194304]{0:T(1024)(128)(4,1)S(1)}, s32[]{:S(2)}) async-start(s8[5242880]{0:T(1024)(128)(4,1)} %bitcast.97), calls=%async_computation.10 | async-start | bytes 8388608
  434.3 7.3 %slice-start.3 = ((s8[5242880]{0:T(1024)(128)(4,1)}), s8[1048576]{0:T(1024)(128)(4,1)S(1)}, s32[]{:S(2)}) async-start(s8[5242880]{0:T(1024)(128)(4,1)} %bitcast.97), calls=%async_computation.11 | async-start | bytes 2097152
  441.6 1.8 copy-start.14
  441.6 2.6 copy-start.19
  447.6 0.8 copy-start.33
  447.6 0.9 copy-start.27
  447.6 73.5 %copy-start.40 = (f32[1024]{0:T(1024)S(1)}, f32[1024]{0:T(1024)}, u32[]{:S(2)}) copy-start(f32[1024]{0:T(1024)} %param.18) | copy-start | bytes 12292
  521.2 7.5 %copy-start.41 = (bf16[1024]{0:T(1024)(128)(2,1)S(1)}, bf16[1024]{0:T(1024)(128)(2,1)}, u32[]{:S(2)}) copy-start(bf16[1024]{0:T(1024)(128)(2,1)} %get-tuple-element.35) | copy-start | bytes 6148
  521.2 7.5 %copy-start.42 = (bf16[1024]{0:T(1024)(128)(2,1)S(1)}, bf16[1024]{0:T(1024)(128)(2,1)}, u32[]{:S(2)}) copy-start(bf16[1024]{0:T(1024)(128)(2,1)} %get-tuple-element.46) | copy-start | bytes 6148
  521.2 7.5 %copy-start.43 = (bf16[1024]{0:T(1024)(128)(2,1)S(1)}, bf16[1024]{0:T(1024)(128)(2,1)}, u32[]{:S(2)}) copy-start(bf16[1024]{0:T(1024)(128)(2,1)} %get-tuple-element.14) | copy-start | bytes 6148
  521.2 7.5 %copy-start.47 = (bf16[1024]{0:T(1024)(128)(2,1)S(1)}, bf16[1024]{0:T(1024)(128)(2,1)}, u32[]{:S(2)}) copy-start(bf16[1024]{0:T(1024)(128)(2,1)} %get-tuple-element.32) | copy-start | bytes 6148
  681.4 5.8 copy-start.17
  683.6 6.0 copy-start.16
Sparse Core Ops, SparseCore 0:
  9.6 57.5 all-gather.2
  68.7 52.9 all-gather.4
  124.7 102.2 all-reduce.6
  261.0 103.0 all-reduce.8
  415.8 103.0 all-reduce.10
  521.7 51.2 reduce-scatter.1
  577.7 103.5 all-reduce.12
where the time goes:
time: 709 us; the launch traced here: 699 us
  waiting for transfers between devices  459 us (65%)
  matrix products  80.6 us (11%)
  other arithmetic  67.6 us (10%)
  local copies, waits for them, and re-layouts  51.6 us (7%)
  blocking collectives  24.7 us (3%)
  between operations  15.3 us (2%)
    psum x1, waiting for transfers between devices, per_device(): lax.psum(attn_part.astype(jnp.bfloat16), 'tensor').astype(jnp.float32)  105 us
    psum x1, waiting for transfers between devices, per_device(): lax.psum(grad_w_qkv.astype(jnp.bfloat16), 'dp').astype(jnp.float32)  104 us
    psum x1, waiting for transfers between devices, per_device(): lax.psum(hidden_part.astype(jnp.bfloat16), 'tensor').astype(jnp.float32)  102 us
    psum x1, waiting for transfers between devices, per_device(): lax.psum(normed_part.astype(jnp.bfloat16), 'tensor').astype(jnp.float32)  67.8 us
    all_gather x1, waiting for transfers between devices, per_device(): lax.all_gather(images, 'tensor', axis=2, tiled=True)  54.3 us
    psum x1, blocking collectives, per_device(): lax.psum(grad_norm1_gain.astype(jnp.bfloat16), 'dp').astype(jnp.float32)  24.7 us
    unnamed x118, local copies, waits for them, and re-layouts  20.9 us
    dot_general x1, matrix products, per_device(): jnp.einsum('rd,fd->rf', grad_ff, w_fc2, preferred_element_type=jnp.float32)  16.8 us
  transfers between devices with their start and end apart: 7, of which 7 were waited for; matrix products, arithmetic and copies ran while one was open for 14% of the time, Pallas kernels for 0%

commit v1 on v0

--- a/solution.py
+++ b/solution.py
@@ -36,6 +36,48 @@
 
 def exact_gelu(values):
     return jax.nn.gelu(values, approximate=False)
+
+
+def swap_with(values, axis, size, stride):
+    return lax.ppermute(values, axis, [(i, i ^ stride) for i in range(size)])
+
+
+def halving_sum(blocks, axis, size):
+    me = lax.axis_index(axis)
+    steps = size.bit_length() - 1
+    assert 1 << steps == size
+    held = [block.astype(jnp.float32) for block in blocks]
+    for step in range(steps):
+        bit = (me >> step) & 1
+        kept, given = [], []
+        for block in held:
+            half = block.shape[0] // 2
+            kept.append(lax.dynamic_slice_in_dim(block, bit * half, half, 0))
+            given.append(lax.dynamic_slice_in_dim(block, (1 - bit) * half, half, 0).astype(jnp.bfloat16))
+        got = swap_with(tuple(given), axis, size, 1 << step)
+        held = [mine + theirs.astype(jnp.float32) for mine, theirs in zip(kept, got)]
+    held = [block.astype(jnp.bfloat16) for block in held]
+    for step in reversed(range(steps)):
+        bit = (me >> step) & 1
+        got = swap_with(tuple(held), axis, size, 1 << step)
+        held = [
+            jnp.where(bit == 0, jnp.concatenate([mine, theirs]), jnp.concatenate([theirs, mine]))
+            for mine, theirs in zip(held, got)
+        ]
+    return [block.astype(jnp.float32) for block in held]
+
+
+def doubling_sum(values, axis, size):
+    steps = size.bit_length() - 1
+    assert 1 << steps == size
+    values = [value.astype(jnp.bfloat16) for value in values]
+    for step in range(steps):
+        got = swap_with(tuple(values), axis, size, 1 << step)
+        values = [
+            (mine.astype(jnp.float32) + theirs.astype(jnp.float32)).astype(jnp.bfloat16)
+            for mine, theirs in zip(values, got)
+        ]
+    return [value.astype(jnp.float32) for value in values]
 
 
 def per_device(
@@ -102,14 +144,7 @@
     normed2 = normed2.astype(jnp.bfloat16)
     pre_act = jnp.dot(normed2, w_fc1, preferred_element_type=jnp.float32) + fc1_bias
     activated = exact_gelu(pre_act).astype(jnp.bfloat16)
-    ff_part = jnp.dot(activated, w_fc2, preferred_element_type=jnp.float32)
-    ff_share = lax.psum_scatter(
-        ff_part.astype(jnp.bfloat16), "tensor", scatter_dimension=1, tiled=True
-    ).astype(jnp.float32)
-    middle_cols = lax.dynamic_slice_in_dim(middle, first_col, col_count, 1)
-    bias_cols = lax.dynamic_slice_in_dim(fc2_bias, first_col, col_count, 0)
-    output = ((middle_cols + ff_share + bias_cols) * keep_rows).astype(jnp.bfloat16)
-    output = output.reshape(images_here, slot_count, col_count)
+    ff_part = jnp.dot(activated, w_fc2, preferred_element_type=jnp.float32).astype(jnp.bfloat16)
     grad_out = full_cot.reshape(row_count, model_width).astype(jnp.float32) * keep_rows
     grad_ff = grad_out.astype(jnp.bfloat16)
     grad_fc2_bias = jnp.sum(grad_ff, axis=0, dtype=jnp.float32)
@@ -121,12 +156,30 @@
     grad_w_fc1 = jnp.einsum("rd,rf->df", normed2, grad_pre, preferred_element_type=jnp.float32)
     hidden_part = jnp.einsum("rf,df->rd", grad_pre, w_fc1, preferred_element_type=jnp.float32)
     grad_normed2 = lax.psum(hidden_part.astype(jnp.bfloat16), "tensor").astype(jnp.float32)
+    ff_part, grad_normed2 = lax.optimization_barrier((ff_part, grad_normed2))
+    ff_share = lax.psum_scatter(ff_part, "tensor", scatter_dimension=1, tiled=True).astype(
+        jnp.float32
+    )
+    middle_cols = lax.dynamic_slice_in_dim(middle, first_col, col_count, 1)
+    bias_cols = lax.dynamic_slice_in_dim(fc2_bias, first_col, col_count, 0)
+    output = ((middle_cols + ff_share + bias_cols) * keep_rows).astype(jnp.bfloat16)
+    output = output.reshape(images_here, slot_count, col_count)
+    dp_size = lax.axis_size("dp")
+    tensor_size = lax.axis_size("tensor")
     grad_norm2_gain = jnp.sum(grad_normed2 * unit2, axis=0)
     grad_norm2_shift = jnp.sum(grad_normed2, axis=0)
     grad_middle = grad_out + norm_back(grad_normed2, unit2, inverse2, norm2_gain)
     grad_attn = grad_middle.astype(jnp.bfloat16)
     grad_proj_bias = jnp.sum(grad_attn, axis=0, dtype=jnp.float32)
     grad_w_proj = jnp.einsum("rc,rd->cd", mixed_rows, grad_attn, preferred_element_type=jnp.float32)
+    grad_w_fc1, grad_w_fc2, grad_w_proj = halving_sum(
+        [grad_w_fc1, grad_w_fc2, grad_w_proj], "dp", dp_size
+    )
+    (grad_fc1_bias, grad_fc2_bias, grad_proj_bias, grad_norm2_gain, grad_norm2_shift) = doubling_sum(
+        [grad_fc1_bias, grad_fc2_bias, grad_proj_bias, grad_norm2_gain, grad_norm2_shift],
+        "dp",
+        dp_size,
+    )
     grad_mixed = jnp.einsum(
         "rd,cd->rc", grad_attn, w_proj, preferred_element_type=jnp.float32
     ).astype(jnp.bfloat16)
@@ -157,43 +210,49 @@
     bias_sums = jnp.sum(grad_qkv, axis=0, dtype=jnp.float32).reshape(3, local_width)
     grad_qv_bias = jnp.stack([bias_sums[0], bias_sums[2]])
     grad_w_qkv = jnp.einsum("rd,rc->dc", normed1, grad_qkv, preferred_element_type=jnp.float32)
+    (grad_w_qkv,) = halving_sum([grad_w_qkv], "dp", dp_size)
     grad_w_qkv = grad_w_qkv.reshape(model_width, 3, local_width)
-    normed_part = jnp.einsum("rc,dc->rd", grad_qkv, w_flat, preferred_element_type=jnp.float32)
-    grad_normed1 = lax.psum(normed_part.astype(jnp.bfloat16), "tensor").astype(jnp.float32)
-    grad_norm1_gain = jnp.sum(grad_normed1 * unit1, axis=0)
-    grad_norm1_shift = jnp.sum(grad_normed1, axis=0)
-    grad_full = grad_middle + norm_back(grad_normed1, unit1, inverse1, norm1_gain)
-    grad_input = lax.dynamic_slice_in_dim(grad_full, first_col, col_count, 1) * keep_rows
+    normed_part = jnp.einsum(
+        "rc,dc->rd", grad_qkv, w_flat, preferred_element_type=jnp.float32
+    ).astype(jnp.bfloat16)
+    output, normed_part = lax.optimization_barrier((output, normed_part))
+    grad_normed1 = lax.psum_scatter(
+        normed_part, "tensor", scatter_dimension=1, tiled=True
+    ).astype(jnp.float32)
+    term = normed_part.astype(jnp.float32)
+    term_gain = term * norm1_gain
+    first_stat = jnp.sum(term_gain, axis=1)
+    second_stat = jnp.sum(term_gain * unit1, axis=1)
+    norm1_terms = jnp.stack([jnp.sum(term * unit1, axis=0), jnp.sum(term, axis=0)])
+    first_stat, second_stat, norm1_terms = doubling_sum(
+        [first_stat, second_stat, norm1_terms], "tensor", tensor_size
+    )
+    norm1_sums, grad_qv_bias = doubling_sum([norm1_terms, grad_qv_bias], "dp", dp_size)
+    first_mean = first_stat / model_width
+    second_mean = second_stat / model_width
+    unit1_cols = lax.dynamic_slice_in_dim(unit1, first_col, col_count, 1)
+    gain1_cols = lax.dynamic_slice_in_dim(norm1_gain, first_col, col_count, 0)
+    input_part = inverse1 * (
+        grad_normed1 * gain1_cols - first_mean[:, None] - unit1_cols * second_mean[:, None]
+    )
+    middle_grad_cols = lax.dynamic_slice_in_dim(grad_middle, first_col, col_count, 1)
+    grad_input = (middle_grad_cols + input_part) * keep_rows
     input_grad = grad_input.astype(jnp.bfloat16).reshape(images_here, slot_count, col_count)
-    summed = (
-        lax.psum(grad_norm1_gain.astype(jnp.bfloat16), "dp").astype(jnp.float32),
-        lax.psum(grad_norm1_shift.astype(jnp.bfloat16), "dp").astype(jnp.float32),
-        lax.psum(grad_w_qkv.astype(jnp.bfloat16), "dp").astype(jnp.float32),
-        lax.psum(grad_qv_bias.astype(jnp.bfloat16), "dp").astype(jnp.float32),
-        lax.psum(grad_w_proj.astype(jnp.bfloat16), "dp").astype(jnp.float32),
-        lax.psum(grad_proj_bias.astype(jnp.bfloat16), "dp").astype(jnp.float32),
-        lax.psum(grad_norm2_gain.astype(jnp.bfloat16), "dp").astype(jnp.float32),
-        lax.psum(grad_norm2_shift.astype(jnp.bfloat16), "dp").astype(jnp.float32),
-        lax.psum(grad_w_fc1.astype(jnp.bfloat16), "dp").astype(jnp.float32),
-        lax.psum(grad_fc1_bias.astype(jnp.bfloat16), "dp").astype(jnp.float32),
-        lax.psum(grad_w_fc2.astype(jnp.bfloat16), "dp").astype(jnp.float32),
-        lax.psum(grad_fc2_bias.astype(jnp.bfloat16), "dp").astype(jnp.float32),
-    )
     return (
         output,
         input_grad,
-        summed[0],
-        summed[1],
-        summed[2],
-        summed[3],
-        summed[4],
-        summed[5],
-        summed[6],
-        summed[7],
-        summed[8],
-        summed[9],
-        summed[10],
-        summed[11],
+        norm1_sums[0],
+        norm1_sums[1],
+        grad_w_qkv,
+        grad_qv_bias,
+        grad_w_proj,
+        grad_proj_bias,
+        grad_norm2_gain,
+        grad_norm2_shift,
+        grad_w_fc1,
+        grad_fc1_bias,
+        grad_w_fc2,
+        grad_fc2_bias,
     )
 
 

time: 709 us -> 568 us (0.80)
  waiting for transfers between devices: 459 us -> 261 us
  starting transfers between devices: 0.53 us -> 46.3 us
  blocking collectives: 24.7 us -> 0 us
  other arithmetic: 67.6 us -> 92.1 us
  local copies, waits for them, and re-layouts: 51.6 us -> 64.3 us
    psum x2 -> x0, waiting for transfers between devices: 172 us -> none  [the longest x1 104 us: per_device(): lax.psum(grad_w_qkv.astype(jnp.bfloat16), 'dp').astype(jnp.float32)]
    ppermute x0 -> x51, waiting for transfers between devices: none -> 61.5 us  [swap_with(): return lax.ppermute(values, axis, [(i, i ^ stride) for i in range(size)])]
    psum x1, waiting for transfers between devices: 102 us -> 44.2 us  [per_device(): lax.psum(hidden_part.astype(jnp.bfloat16), 'tensor').astype(jnp.float32)]
    ppermute x0 -> x51, starting transfers between devices: none -> 46.1 us  [swap_with(): return lax.ppermute(values, axis, [(i, i ^ stride) for i in range(size)])]
    psum x1 -> x0, blocking collectives: 24.7 us -> none  [per_device(): lax.psum(grad_norm1_gain.astype(jnp.bfloat16), 'dp').astype(jnp.float32)]
    psum x1, waiting for transfers between devices: 105 us -> 90.1 us  [per_device(): lax.psum(attn_part.astype(jnp.bfloat16), 'tensor').astype(jnp.float32)]
    reduce_scatter x1 -> x2, waiting for transfers between devices: 14.9 us -> 0.01 us  [the longest x1 0.01 us: per_device(): lax.psum_scatter(ff_part, 'tensor', scatter_dimension=1, tiled=True)]
    convert_element_type x12 -> x35, other arithmetic: 15.5 us -> 28 us  [the longest x4 12.9 us: halving_sum(): return [block.astype(jnp.float32) for block in held]]
  transfers between devices with their start and end apart: 7 -> 57, of which waited for: 7 -> 24; matrix products, arithmetic and copies ran while one was open for 14% -> 35% of each run, Pallas kernels for 0% -> 0%
where the time goes in v1:
time: 568 us; the launch traced here: 558 us
  waiting for transfers between devices  261 us (46%)
  other arithmetic  92.1 us (16%)
  matrix products  78.6 us (14%)
  local copies, waits for them, and re-layouts  64.3 us (11%)
  starting transfers between devices  46.3 us (8%)
  between operations  15.6 us (3%)
    psum x1, waiting for transfers between devices, per_device(): lax.psum(attn_part.astype(jnp.bfloat16), 'tensor').astype(jnp.float32)  90.1 us
    ppermute x51, waiting for transfers between devices, swap_with(): return lax.ppermute(values, axis, [(i, i ^ stride) for i in range(size)])  61.5 us
    all_gather x1, waiting for transfers between devices, per_device(): lax.all_gather(images, 'tensor', axis=2, tiled=True)  54.3 us
    ppermute x51, starting transfers between devices, swap_with(): return lax.ppermute(values, axis, [(i, i ^ stride) for i in range(size)])  46.1 us
    psum x1, waiting for transfers between devices, per_device(): lax.psum(hidden_part.astype(jnp.bfloat16), 'tensor').astype(jnp.float32)  44.2 us
    unnamed x110, local copies, waits for them, and re-layouts  18.4 us
    dot_general x1, matrix products, per_device(): jnp.einsum('rd,fd->rf', grad_ff, w_fc2, preferred_element_type=jnp.float32)  16.9 us
    convert_element_type x4, other arithmetic, halving_sum(): return [block.astype(jnp.float32) for block in held]  12.9 us
  transfers between devices with their start and end apart: 57, of which 24 were waited for; matrix products, arithmetic and copies ran while one was open for 35% of the time, Pallas kernels for 0%

profile of v1, /device:TPU:0, one launch (start us, length us, event | category | flops | bytes accessed | tf_op | source)
XLA Modules:
  0.0 557.9 jit_solution(11959580105190340628)
XLA Ops:
  10.2 2.6 copy.46
  12.8 54.3 %all-gather.3.cloned.1.call-done = bf16[4,320,1024]{2,1,0:T(8,128)(2,1)} async-done(((bf16[4,320,256]{2,1,0:T(8,128)(2,1)}), bf16[4,320,1024]{2,1,0:T(8,128)(2,1)}) %all-gather.3.cloned.1.call-update) | async-done | bytes 2621456 | tf_op jit(solution)/shard_map/all_gather | solution.py:108
  67.2 2.6 fusion.13
  69.8 2.8 multiply_reduce_fusion.4
  75.4 3.5 add_convert_fusion.3
  78.9 6.7 %reshape.273 = bf16[4,320,3,4,64]{4,3,2,1,0:T(4,128)(2,1)} reshape(bf16[1280,768]{1,0:T(8,128)(2,1)} %add_convert_fusion.3) | data formatting | bytes 3932160 | tf_op jit(solution)/shard_map/reshape | solution.py:122
  85.6 3.9 fusion.64
  89.5 2.4 copy.76
  91.9 2.5 copy.77
  94.4 3.2 copy.78
  97.6 3.2 fusion.19
  102.8 2.4 fusion.28
  106.8 2.1 reshape.266
  108.8 3.4 convolution_convert_fusion.1
  112.3 9.4 %all-gather.5.cloned.1.call-done = bf16[4,320,1024]{2,1,0:T(8,128)(2,1)} async-done(((bf16[4,320,256]{2,1,0:T(8,128)(2,1)}), bf16[4,320,1024]{2,1,0:T(8,128)(2,1)}) %all-gather.5.cloned.1.call-update) | async-done | bytes 2621456 | tf_op jit(solution)/shard_map/all_gather | solution.py:109
  121.8 2.3 fusion.20
  136.9 90.1 %all-reduce.3.cloned.1.call-done = bf16[1280,1024]{1,0:T(8,128)(2,1)} async-done(((bf16[1280,1024]{1,0:T(8,128)(2,1)}), bf16[1280,1024]{1,0:T(8,128)(2,1)}) %all-reduce.3.cloned.1.call-update) | async-done | bytes 2621456 | tf_op jit(solution)/shard_map/psum | solution.py:140
  227.0 5.0 fusion.63
  232.7 2.5 copy-done.45
  235.2 3.1 fusion.59
  238.3 16.9 %fusion.60 = (bf16[1024]{0:T(1024)(128)(2,1)}, bf16[1280,1024]{1,0:T(8,128)(2,1)}, f32[1280,1024]{1,0:T(8,128)S(1)}) fusion(f32[1280,1024]{1,0:T(8,128)S(1)} %fusion.59, f32[1024]{0:T(1024)S(1)} %copy-done.42, bf16[1280,1024]{1,0:T(8,128)(2,1)S(1)} %get-tuple-element.44, bf16[1024,1024]{1,0:T(8,128)(2,1)S(1)} %copy-done), kind=kOutput, calls=%fused_computation.180 | convolution fusion | flops 2781346816 | bytes 17831936 | tf_op jit(solution)/shard_map/rd,fd->rf/dot_general | solution.py:152
  256.6 2.9 fusion.68
  260.9 5.2 fusion.58
  266.1 4.2 convolution_convert_fusion.2
  270.9 2.7 dynamic-slice_convert_fusion.1
  273.6 6.3 %convolution_convert_fusion.3 = bf16[1280,1024]{1,0:T(8,128)(2,1)} fusion(bf16[1280,1024]{1,0:T(8,128)(2,1)} %copy-done.13, bf16[1024,1024]{1,0:T(8,128)(2,1)S(1)} %copy-done), kind=kOutput, calls=%fused_computation.56 | convolution fusion | flops 2685665280 | bytes 7340032 | tf_op jit(solution)/shard_map/dot_general | solution.py:147
  279.9 2.4 convert_add_fusion
  288.3 9.0 %collective-permute-done.43 = bf16[256,1024]{1,0:T(8,128)(2,1)S(1)} collective-permute-done((bf16[256,1024]{1,0:T(8,128)(2,1)S(1)}, bf16[256,1024]{1,0:T(8,128)(2,1)S(1)}, u32[]{:S(2)}, u32[]{:S(2)}) %collective-permute-start.43) | collective-permute-done | bytes 524320 | tf_op jit(solution)/shard_map/ppermute | solution.py:42
  298.8 9.4 %collective-permute-done.34 = bf16[256,1024]{1,0:T(8,128)(2,1)S(1)} collective-permute-done((bf16[256,1024]{1,0:T(8,128)(2,1)S(1)}, bf16[256,1024]{1,0:T(8,128)(2,1)S(1)}, u32[]{:S(2)}, u32[]{:S(2)}) %collective-permute-start.34) | collective-permute-done | bytes 524320 | tf_op jit(solution)/shard_map/ppermute | solution.py:42
  311.9 5.7 %collective-permute-done.35 = bf16[128,1024]{1,0:T(8,128)(2,1)S(1)} collective-permute-done((bf16[128,1024]{1,0:T(8,128)(2,1)S(1)}, bf16[128,1024]{1,0:T(8,128)(2,1)S(1)}, u32[]{:S(2)}, u32[]{:S(2)}) %collective-permute-start.35) | collective-permute-done | bytes 262176 | tf_op jit(solution)/shard_map/ppermute | solution.py:42
  319.6 3.7 collective-permute-done.45
  325.5 2.3 collective-permute-done.36
  329.9 44.2 %all-reduce.5.cloned.1.call-done = bf16[1280,1024]{1,0:T(8,128)(2,1)} async-done(((bf16[1280,1024]{1,0:T(8,128)(2,1)}), bf16[1280,1024]{1,0:T(8,128)(2,1)}) %all-reduce.5.cloned.1.call-update) | async-done | bytes 2621456 | tf_op jit(solution)/shard_map/psum | solution.py:158
  374.1 2.5 convert_element_type.548
  376.7 5.3 multiply_reduce_fusion.1
  382.0 3.0 convert_reduce_fusion
  385.1 2.3 fusion.51
  390.2 3.2 copy.54
  393.4 6.4 %fusion.29 = bf16[4,320,1,4,64]{1,4,3,0,2:T(8,128)(2,1)} fusion(bf16[4,320,4,64]{1,3,2,0:T(8,128)(2,1)} %copy.54, f32[4,4,320]{2,1,0:T(4,128)} %bitcast.109, f32[4,4,320,320]{2,3,1,0:T(8,128)} %copy-done.1, pred[4,320]{1,0:T(4,128)(4,1)S(1)} %copy-done.34), kind=kOutput, calls=%fused_computation.80 | convolution fusion | flops 216596480 | bytes 7886080 | tf_op jit(solution)/shard_map/bhqk,bqhe->bkhe/dot_general | solution.py:189
  399.8 5.4 multiply_reduce_fusion
  405.2 2.7 multiply_convert_fusion
  408.0 2.2 fusion.33
  412.7 3.2 fusion.62
  416.1 5.3 copy.59
  421.5 4.7 convert_element_type.555
  428.0 4.7 fusion.69
  435.3 3.8 convolution_convert_fusion
  439.6 2.2 maximum_select_fusion.4
  441.9 3.1 maximum_select_fusion.3
  461.6 3.4 collective-permute-done.19
  472.1 3.5 collective-permute-done.10
  478.1 2.6 multiply_convert_fusion.6
  480.7 3.0 collective-permute-done.11
  498.8 3.2 collective-permute-done.13
  504.9 4.4 fusion.22
  509.4 5.3 fusion.21
  517.5 2.3 copy.66
  519.8 2.2 reduce.7
  522.0 6.8 %fusion.5 = (bf16[1024]{0:T(1024)(128)(2,1)S(1)}, bf16[1280]{0:T(1024)(128)(2,1)S(1)}, bf16[1280]{0:T(1024)(128)(2,1)S(1)}, f32[1280,1024]{1,0:T(8,128)}) fusion(bf16[1280,1024]{1,0:T(8,128)(2,1)} %convolution_convert_fusion, f32[1280]{0:T(1024)S(1)} %copy-done.31, f32[1280]{0:T(1024)} %div.43, f32[1280]{0:T(1024)S(1)} %reshape.271, ...), kind=kLoop, calls=%fused_computation.14 | loop fusion | flops 14414336 | bytes 10512384 | tf_op jit(solution)/shard_map/reduce_sum | solution.py:226
  529.0 2.0 fusion.23
  531.0 2.0 collective-permute-start.2
  540.7 2.5 collective-permute-done.7
  543.3 3.6 collective-permute-done.8
  547.4 3.2 multiply_convert_fusion.5
  (303 shorter events, 109.5 us)
Async XLA Ops:
  7.2 231.1 %copy-start = (bf16[1024,1024]{1,0:T(8,128)(2,1)S(1)}, bf16[1024,1024]{1,0:T(8,128)(2,1)}, u32[]{:S(2)}) copy-start(bf16[1024,1024]{1,0:T(8,128)(2,1)} %param.28) | copy-start | bytes 6291460
  7.2 65.4 %copy-start.35 = (f32[1024]{0:T(1024)S(1)}, f32[1024]{0:T(1024)}, u32[]{:S(2)}) copy-start(f32[1024]{0:T(1024)} %param.18) | copy-start | bytes 12292
  7.2 65.3 %copy-start.41 = (f32[1024]{0:T(1024)S(1)}, f32[1024]{0:T(1024)}, u32[]{:S(2)}) copy-start(f32[1024]{0:T(1024)} %param.19) | copy-start | bytes 12292
  7.2 60.0 %all-gather.3.cloned.1.call-start = ((), (), s32[]{:S(2)}) async-start(), calls=%async_computation.2 | async-start | bytes 3276800 | tf_op jit(solution)/shard_map/all_gather | solution.py:108
  8.0 113.8 %all-gather.5.cloned.1.call-start = ((), (), s32[]{:S(2)}) async-start(), calls=%async_computation.4 | async-start | bytes 3276800 | tf_op jit(solution)/shard_map/all_gather | solution.py:109
  8.7 218.3 %all-reduce.3.cloned.1.call-start = ((), (), s32[]{:S(2)}) async-start(), calls=%async_computation.3 | async-start | bytes 5242880 | tf_op jit(solution)/shard_map/psum | solution.py:140
  10.2 92.5 %copy-start.33 = (pred[4,320]{1,0:T(4,128)(4,1)}, pred[4,320]{1,0:T(4,128)(4,1)S(1)}, u32[]{:S(2)}) copy-start(pred[4,320]{1,0:T(4,128)(4,1)S(1)} %get-tuple-element.49) | copy-start | bytes 3844
  112.3 261.8 %all-reduce.5.cloned.1.call-start = ((), (), s32[]{:S(2)}) async-start(), calls=%async_computation.5 | async-start | bytes 5242880 | tf_op jit(solution)/shard_map/psum | solution.py:158
  124.1 1.2 collective-permute-start.48
  125.9 4.2 collective-permute-start.49
  130.8 5.6 collective-permute-start.50
  232.0 28.9 %copy-start.2 = (f32[1280,1024]{1,0:T(8,128)}, f32[1280,1024]{1,0:T(8,128)S(1)}, u32[]{:S(2)}) copy-start(f32[1280,1024]{1,0:T(8,128)S(1)} %get-tuple-element.37) | copy-start | bytes 15728644
  235.2 25.7 %copy-start.29 = (f32[1280]{0:T(1024)}, f32[1280]{0:T(1024)S(1)}, u32[]{:S(2)}) copy-start(f32[1280]{0:T(1024)S(1)} %add_rsqrt_fusion) | copy-start | bytes 15364
  260.9 19.0 %collective-permute-start.42 = (bf16[512,1024]{1,0:T(8,128)(2,1)}, bf16[512,1024]{1,0:T(8,128)(2,1)}, u32[]{:S(2)}, u32[]{:S(2)}) collective-permute-start(bf16[512,1024]{1,0:T(8,128)(2,1)} %dynamic-slice_convert_fusion), channel_id=1, source_target_pairs={{0,4},{4,0},{8,12},{12,8},{16,20},{20,16},{24,28},{28,24},{1,5},{5... | collective-permute-start | bytes 3145736 | tf_op jit(solution)/shard_map/ppermute | solution.py:42
  270.3 16.0 %collective-permute-start.39 = (bf16[1024]{0:T(1024)(128)(2,1)}, bf16[1024]{0:T(1024)(128)(2,1)}, u32[]{:S(2)}, u32[]{:S(2)}) collective-permute-start(bf16[1024]{0:T(1024)(128)(2,1)} %get-tuple-element.29), channel_id=1, source_target_pairs={{0,4},{4,0},{8,12},{12,8},{16,20},{20,16},{24,28},{28,24},{1,5},{5... | collective-permute-start | bytes 6152 | tf_op jit(solution)/shard_map/ppermute | solution.py:42
  270.8 207.2 %reduce-scatter.3.cloned.1.call-start = ((), (), s32[]{:S(2)}) async-start(), calls=%async_computation.6 | async-start | bytes 3276800 | tf_op jit(solution)/shard_map/reduce_scatter | solution.py:160
  273.6 10.1 %collective-permute-start.33 = (bf16[512,1024]{1,0:T(8,128)(2,1)}, bf16[512,1024]{1,0:T(8,128)(2,1)}, u32[]{:S(2)}, u32[]{:S(2)}) collective-permute-start(bf16[512,1024]{1,0:T(8,128)(2,1)} %dynamic-slice_convert_fusion.1), channel_id=1, source_target_pairs={{0,4},{4,0},{8,12},{12,8},{16,20},{20,16},{24,28},{28,24},{1,5},{5... | collective-permute-start | bytes 3145736 | tf_op jit(solution)/shard_map/ppermute | solution.py:42
  282.4 14.9 %collective-permute-start.43 = (bf16[256,1024]{1,0:T(8,128)(2,1)S(1)}, bf16[256,1024]{1,0:T(8,128)(2,1)S(1)}, u32[]{:S(2)}, u32[]{:S(2)}) collective-permute-start(bf16[256,1024]{1,0:T(8,128)(2,1)S(1)} %dynamic-slice_convert_fusion.3), channel_id=1, source_target_pairs={{0,8},{4,12},{8,0},{12,4},{16,24},{20,28},{24,16},{28,20},{1,9},{5... | collective-permute-start | bytes 1572872 | tf_op jit(solution)/shard_map/ppermute | solution.py:42
  285.5 22.6 %collective-permute-start.34 = (bf16[256,1024]{1,0:T(8,128)(2,1)S(1)}, bf16[256,1024]{1,0:T(8,128)(2,1)S(1)}, u32[]{:S(2)}, u32[]{:S(2)}) collective-permute-start(bf16[256,1024]{1,0:T(8,128)(2,1)S(1)} %dynamic-slice_convert_fusion.4), channel_id=1, source_target_pairs={{0,8},{4,12},{8,0},{12,4},{16,24},{20,28},{24,16},{28,20},{1,9},{5... | collective-permute-start | bytes 1572872 | tf_op jit(solution)/shard_map/ppermute | solution.py:42
  287.1 22.7 %collective-permute-start.40 = (bf16[1024]{0:T(1024)(128)(2,1)S(1)}, bf16[1024]{0:T(1024)(128)(2,1)S(1)}, u32[]{:S(2)}, u32[]{:S(2)}) collective-permute-start(bf16[1024]{0:T(1024)(128)(2,1)S(1)} %add_convert_fusion.22), channel_id=1, source_target_pairs={{0,8},{4,12},{8,0},{12,4},{16,24},{20,28},{24,16},{28,20},{1,9},{5... | collective-permute-start | bytes 6152 | tf_op jit(solution)/shard_map/ppermute | solution.py:42
  297.5 13.1 %collective-permute-start.44 = (bf16[128,1024]{1,0:T(8,128)(2,1)S(1)}, bf16[128,1024]{1,0:T(8,128)(2,1)S(1)}, u32[]{:S(2)}, u32[]{:S(2)}) collective-permute-start(bf16[128,1024]{1,0:T(8,128)(2,1)S(1)} %dynamic-slice_convert_fusion.6), channel_id=1, source_target_pairs={{0,16},{4,20},{8,24},{12,28},{16,0},{20,4},{24,8},{28,12},{1,17},{... | collective-permute-start | bytes 786440 | tf_op jit(solution)/shard_map/ppermute | solution.py:42
  308.4 9.2 %collective-permute-start.35 = (bf16[128,1024]{1,0:T(8,128)(2,1)S(1)}, bf16[128,1024]{1,0:T(8,128)(2,1)S(1)}, u32[]{:S(2)}, u32[]{:S(2)}) collective-permute-start(bf16[128,1024]{1,0:T(8,128)(2,1)S(1)} %dynamic-slice_convert_fusion.7), channel_id=1, source_target_pairs={{0,16},{4,20},{8,24},{12,28},{16,0},{20,4},{24,8},{28,12},{1,17},{... | collective-permute-start | bytes 786440 | tf_op jit(solution)/shard_map/ppermute | solution.py:42
  309.7 9.3 %collective-permute-start.41 = (bf16[1024]{0:T(1024)(128)(2,1)S(1)}, bf16[1024]{0:T(1024)(128)(2,1)S(1)}, u32[]{:S(2)}, u32[]{:S(2)}) collective-permute-start(bf16[1024]{0:T(1024)(128)(2,1)S(1)} %add_convert_fusion.21), channel_id=1, source_target_pairs={{0,16},{4,20},{8,24},{12,28},{16,0},{20,4},{24,8},{28,12},{1,17},{... | collective-permute-start | bytes 6152 | tf_op jit(solution)/shard_map/ppermute | solution.py:42
  310.6 12.7 %collective-permute-start.45 = (bf16[128,1024]{1,0:T(8,128)(2,1)S(1)}, bf16[128,1024]{1,0:T(8,128)(2,1)S(1)}, u32[]{:S(2)}, u32[]{:S(2)}) collective-permute-start(bf16[128,1024]{1,0:T(8,128)(2,1)S(1)} %add_convert_fusion.4), channel_id=1, source_target_pairs={{0,16},{4,20},{8,24},{12,28},{16,0},{20,4},{24,8},{28,12},{1,17},{... | collective-permute-start | bytes 786440 | tf_op jit(solution)/shard_map/ppermute | solution.py:42
  317.7 10.1 %collective-permute-start.36 = (bf16[128,1024]{1,0:T(8,128)(2,1)S(1)}, bf16[128,1024]{1,0:T(8,128)(2,1)S(1)}, u32[]{:S(2)}, u32[]{:S(2)}) collective-permute-start(bf16[128,1024]{1,0:T(8,128)(2,1)S(1)} %add_convert_fusion.5), channel_id=1, source_target_pairs={{0,16},{4,20},{8,24},{12,28},{16,0},{20,4},{24,8},{28,12},{1,17},{... | collective-permute-start | bytes 786440 | tf_op jit(solution)/shard_map/ppermute | solution.py:42
  324.2 114.9 %collective-permute-start.46 = (bf16[256,1024]{1,0:T(8,128)(2,1)}, bf16[256,1024]{1,0:T(8,128)(2,1)}, u32[]{:S(2)}, u32[]{:S(2)}) collective-permute-start(bf16[256,1024]{1,0:T(8,128)(2,1)} %maximum_select_fusion.9), channel_id=1, source_target_pairs={{0,8},{4,12},{8,0},{12,4},{16,24},{20,28},{24,16},{28,20},{1,9},{5... | collective-permute-start | bytes 1572872 | tf_op jit(solution)/shard_map/ppermute | solution.py:42
  328.7 113.0 %collective-permute-start.37 = (bf16[256,1024]{1,0:T(8,128)(2,1)}, bf16[256,1024]{1,0:T(8,128)(2,1)}, u32[]{:S(2)}, u32[]{:S(2)}) collective-permute-start(bf16[256,1024]{1,0:T(8,128)(2,1)} %maximum_select_fusion.8), channel_id=1, source_target_pairs={{0,8},{4,12},{8,0},{12,4},{16,24},{20,28},{24,16},{28,20},{1,9},{5... | collective-permute-start | bytes 1572872 | tf_op jit(solution)/shard_map/ppermute | solution.py:42
  412.0 135.5 %reduce-scatter.5.cloned.1.call-start = ((), (), s32[]{:S(2)}) async-start(), calls=%async_computation.7 | async-start | bytes 3276800 | tf_op jit(solution)/shard_map/reduce_scatter | solution.py:219
  412.0 33.4 %collective-permute-start.24 = (bf16[1024]{0:T(1024)(128)(2,1)S(1)}, bf16[1024]{0:T(1024)(128)(2,1)S(1)}, u32[]{:S(2)}, u32[]{:S(2)}) collective-permute-start(bf16[1024]{0:T(1024)(128)(2,1)S(1)} %copy-done.40), channel_id=1, source_target_pairs={{0,4},{4,0},{8,12},{12,8},{16,20},{20,16},{24,28},{28,24},{1,5},{5... | collective-permute-start | bytes 6152 | tf_op jit(solution)/shard_map/ppermute | solution.py:42
  412.1 33.4 %collective-permute-start.27 = (bf16[1024]{0:T(1024)(128)(2,1)S(1)}, bf16[1024]{0:T(1024)(128)(2,1)S(1)}, u32[]{:S(2)}, u32[]{:S(2)}) collective-permute-start(bf16[1024]{0:T(1024)(128)(2,1)S(1)} %copy-done.39), channel_id=1, source_target_pairs={{0,4},{4,0},{8,12},{12,8},{16,20},{20,16},{24,28},{28,24},{1,5},{5... | collective-permute-start | bytes 6152 | tf_op jit(solution)/shard_map/ppermute | solution.py:42
  412.6 36.6 %collective-permute-start.30 = (bf16[1024]{0:T(1024)(128)(2,1)S(1)}, bf16[1024]{0:T(1024)(128)(2,1)S(1)}, u32[]{:S(2)}, u32[]{:S(2)}) collective-permute-start(bf16[1024]{0:T(1024)(128)(2,1)S(1)} %copy-done.38), channel_id=1, source_target_pairs={{0,4},{4,0},{8,12},{12,8},{16,20},{20,16},{24,28},{28,24},{1,5},{5... | collective-permute-start | bytes 6152 | tf_op jit(solution)/shard_map/ppermute | solution.py:42
  439.2 28.0 %copy-start.20 = (f32[1024,768]{0,1:T(8,128)S(1)}, f32[1024,768]{0,1:T(8,128)}, u32[]{:S(2)}) copy-start(f32[1024,768]{0,1:T(8,128)} %copy-done.19) | copy-start | bytes 9437188
  439.2 18.9 %collective-permute-start.18 = (bf16[128,1024]{1,0:T(8,128)(2,1)}, bf16[128,1024]{1,0:T(8,128)(2,1)S(1)}, u32[]{:S(2)}, u32[]{:S(2)}) collective-permute-start(bf16[128,1024]{1,0:T(8,128)(2,1)} %dynamic-slice_convert_fusion.8), channel_id=1, source_target_pairs={{0,4},{4,0},{8,12},{12,8},{16,20},{20,16},{24,28},{28,24},{1,5},{5... | collective-permute-start | bytes 786440 | tf_op jit(solution)/shard_map/ppermute | solution.py:42
  441.8 3.2 collective-permute-start.15
  445.0 21.7 %collective-permute-start.9 = (bf16[512,768]{0,1:T(8,128)(2,1)}, bf16[512,768]{0,1:T(8,128)(2,1)S(1)}, u32[]{:S(2)}, u32[]{:S(2)}) collective-permute-start(bf16[512,768]{0,1:T(8,128)(2,1)} %dynamic-slice_convert_fusion.2), channel_id=1, source_target_pairs={{0,4},{4,0},{8,12},{12,8},{16,20},{20,16},{24,28},{28,24},{1,5},{5... | collective-permute-start | bytes 2359304 | tf_op jit(solution)/shard_map/ppermute | solution.py:42
  445.4 59.5 %collective-permute-start.47 = (bf16[512,1024]{1,0:T(8,128)(2,1)S(1)}, bf16[512,1024]{1,0:T(8,128)(2,1)}, u32[]{:S(2)}, u32[]{:S(2)}) collective-permute-start(bf16[512,1024]{1,0:T(8,128)(2,1)S(1)} %maximum_select_fusion.4), channel_id=1, source_target_pairs={{0,4},{4,0},{8,12},{12,8},{16,20},{20,16},{24,28},{28,24},{1,5},{5... | collective-permute-start | bytes 3145736 | tf_op jit(solution)/shard_map/ppermute | solution.py:42
  445.6 3.6 collective-permute-start.16
  449.2 60.2 %collective-permute-start.38 = (bf16[512,1024]{1,0:T(8,128)(2,1)}, bf16[512,1024]{1,0:T(8,128)(2,1)}, u32[]{:S(2)}, u32[]{:S(2)}) collective-permute-start(bf16[512,1024]{1,0:T(8,128)(2,1)} %maximum_select_fusion.3), channel_id=1, source_target_pairs={{0,4},{4,0},{8,12},{12,8},{16,20},{20,16},{24,28},{28,24},{1,5},{5... | collective-permute-start | bytes 3145736 | tf_op jit(solution)/shard_map/ppermute | solution.py:42
  449.2 3.6 collective-permute-start.17
  452.9 3.6 collective-permute-start.25
  456.4 3.6 collective-permute-start.28
  458.0 9.5 %collective-permute-start.31 = (bf16[1024]{0:T(1024)(128)(2,1)S(1)}, bf16[1024]{0:T(1024)(128)(2,1)S(1)}, u32[]{:S(2)}, u32[]{:S(2)}) collective-permute-start(bf16[1024]{0:T(1024)(128)(2,1)S(1)} %add_convert_fusion.25), channel_id=1, source_target_pairs={{0,8},{4,12},{8,0},{12,4},{16,24},{20,28},{24,16},{28,20},{1,9},{5... | collective-permute-start | bytes 6152 | tf_op jit(solution)/shard_map/ppermute | solution.py:42
  460.0 5.0 collective-permute-start.19
  465.0 21.7 %collective-permute-start.26 = (bf16[1024]{0:T(1024)(128)(2,1)S(1)}, bf16[1024]{0:T(1024)(128)(2,1)}, u32[]{:S(2)}, u32[]{:S(2)}) collective-permute-start(bf16[1024]{0:T(1024)(128)(2,1)S(1)} %add_convert_fusion.30), channel_id=1, source_target_pairs={{0,16},{4,20},{8,24},{12,28},{16,0},{20,4},{24,8},{28,12},{1,17},{... | collective-permute-start | bytes 6152 | tf_op jit(solution)/shard_map/ppermute | solution.py:42
  466.6 4.3 collective-permute-start.20
  467.5 8.0 %collective-permute-start.10 = (bf16[256,768]{0,1:T(8,128)(2,1)S(1)}, bf16[256,768]{0,1:T(8,128)(2,1)S(1)}, u32[]{:S(2)}, u32[]{:S(2)}) collective-permute-start(bf16[256,768]{0,1:T(8,128)(2,1)S(1)} %dynamic-slice_convert_fusion.5), channel_id=1, source_target_pairs={{0,8},{4,12},{8,0},{12,4},{16,24},{20,28},{24,16},{28,20},{1,9},{5... | collective-permute-start | bytes 1179656 | tf_op jit(solution)/shard_map/ppermute | solution.py:42
  471.0 23.2 %collective-permute-start.29 = (bf16[1024]{0:T(1024)(128)(2,1)S(1)}, bf16[1024]{0:T(1024)(128)(2,1)}, u32[]{:S(2)}, u32[]{:S(2)}) collective-permute-start(bf16[1024]{0:T(1024)(128)(2,1)S(1)} %add_convert_fusion.27), channel_id=1, source_target_pairs={{0,16},{4,20},{8,24},{12,28},{16,0},{20,4},{24,8},{28,12},{1,17},{... | collective-permute-start | bytes 6152 | tf_op jit(solution)/shard_map/ppermute | solution.py:42
  476.6 7.1 %collective-permute-start.11 = (bf16[128,768]{0,1:T(8,128)(2,1)S(1)}, bf16[128,768]{0,1:T(8,128)(2,1)S(1)}, u32[]{:S(2)}, u32[]{:S(2)}) collective-permute-start(bf16[128,768]{0,1:T(8,128)(2,1)S(1)} %dynamic-slice_convert_fusion.9), channel_id=1, source_target_pairs={{0,16},{4,20},{8,24},{12,28},{16,0},{20,4},{24,8},{28,12},{1,17},{... | collective-permute-start | bytes 589832 | tf_op jit(solution)/shard_map/ppermute | solution.py:42
  483.7 4.5 collective-permute-start.21
  486.7 5.7 %collective-permute-start.12 = (bf16[128,768]{0,1:T(8,128)(2,1)S(1)}, bf16[128,768]{0,1:T(8,128)(2,1)S(1)}, u32[]{:S(2)}, u32[]{:S(2)}) collective-permute-start(bf16[128,768]{0,1:T(8,128)(2,1)S(1)} %add_convert_fusion.6), channel_id=1, source_target_pairs={{0,16},{4,20},{8,24},{12,28},{16,0},{20,4},{24,8},{28,12},{1,17},{... | collective-permute-start | bytes 589832 | tf_op jit(solution)/shard_map/ppermute | solution.py:42
  488.2 9.3 %collective-permute-start.32 = (bf16[1024]{0:T(1024)(128)(2,1)}, bf16[1024]{0:T(1024)(128)(2,1)S(1)}, u32[]{:S(2)}, u32[]{:S(2)}) collective-permute-start(bf16[1024]{0:T(1024)(128)(2,1)} %add_convert_fusion.24), channel_id=1, source_target_pairs={{0,16},{4,20},{8,24},{12,28},{16,0},{20,4},{24,8},{28,12},{1,17},{... | collective-permute-start | bytes 6152 | tf_op jit(solution)/shard_map/ppermute | solution.py:42
  492.4 5.0 collective-permute-start.22
  494.2 7.8 %collective-permute-start.13 = (bf16[256,768]{0,1:T(8,128)(2,1)S(1)}, bf16[256,768]{0,1:T(8,128)(2,1)S(1)}, u32[]{:S(2)}, u32[]{:S(2)}) collective-permute-start(bf16[256,768]{0,1:T(8,128)(2,1)S(1)} %maximum_select_fusion.11), channel_id=1, source_target_pairs={{0,8},{4,12},{8,0},{12,4},{16,24},{20,28},{24,16},{28,20},{1,9},{5... | collective-permute-start | bytes 1179656 | tf_op jit(solution)/shard_map/ppermute | solution.py:42
  497.4 6.4 %collective-permute-start.23 = (bf16[128,1024]{1,0:T(8,128)(2,1)S(1)}, bf16[128,1024]{1,0:T(8,128)(2,1)S(1)}, u32[]{:S(2)}, u32[]{:S(2)}) collective-permute-start(bf16[128,1024]{1,0:T(8,128)(2,1)S(1)} %maximum_select_fusion.12), channel_id=1, source_target_pairs={{0,4},{4,0},{8,12},{12,8},{16,20},{20,16},{24,28},{28,24},{1,5},{5... | collective-permute-start | bytes 786440 | tf_op jit(solution)/shard_map/ppermute | solution.py:42
  503.8 13.6 %collective-permute-start.14 = (bf16[512,768]{0,1:T(8,128)(2,1)}, bf16[512,768]{0,1:T(8,128)(2,1)}, u32[]{:S(2)}, u32[]{:S(2)}) collective-permute-start(bf16[512,768]{0,1:T(8,128)(2,1)} %maximum_select_fusion.6), channel_id=1, source_target_pairs={{0,4},{4,0},{8,12},{12,8},{16,20},{20,16},{24,28},{28,24},{1,5},{5... | collective-permute-start | bytes 2359304 | tf_op jit(solution)/shard_map/ppermute | solution.py:42
  528.9 4.2 collective-permute-start.4
  531.0 3.7 collective-permute-start.2
  533.0 4.7 collective-permute-start
  533.1 4.6 collective-permute-start.5
  534.7 5.9 %collective-permute-start.3 = (bf16[1280]{0:T(1024)(128)(2,1)S(1)}, bf16[1280]{0:T(1024)(128)(2,1)S(1)}, u32[]{:S(2)}, u32[]{:S(2)}) collective-permute-start(bf16[1280]{0:T(1024)(128)(2,1)S(1)} %add_convert_fusion.14), channel_id=1, source_target_pairs={{0,2},{1,3},{2,0},{3,1},{4,6},{5,7},{6,4},{7,5},{8,10},{9,11},{10,... | collective-permute-start | bytes 7688 | tf_op jit(solution)/shard_map/ppermute | solution.py:42
  537.6 1.8 collective-permute-start.6
  537.8 5.5 collective-permute-start.1
  539.5 3.7 collective-permute-start.7
  543.2 3.7 collective-permute-start.8
  (46 other events, 221.1 us)
Sparse Core Ops, SparseCore 0:
  9.6 57.5 all-gather.2
  68.7 52.9 all-gather.4
  124.7 102.2 all-reduce.2
  271.0 103.0 all-reduce.4
  412.1 51.3 reduce-scatter.2
  480.8 50.0 reduce-scatter.4
